TPU v7x, 32 devices: a whole 2x2x4 slice. The times are simulated.
32 devices in a mesh: section: 4 (over y, core), tp: 8 (over z, x).
Axes of the slice: x: 2, y: 2, z: 4, core: 2. Of those that a mesh axis runs over, the one named last changes fastest.
Arguments:
- token_ids: int32 [2, 128], replicated, may hold values from 0 to 65535
- alpha_num: int32 [1], replicated, may hold values from 3 to 7
- embed_table: bfloat16 [65536, 8192], P('section', 'tp'), may hold values from -6 to 6
- norm_gain: float32 [4, 8192], P('section'), may hold values from 0.5 to 1.5
- w_query: bfloat16 [4, 8192, 4096], P('section', None, 'tp'), may hold values from -4 to 4
- w_key: bfloat16 [4, 8192, 512], P('section', None, 'tp'), may hold values from -4 to 4
- w_value: bfloat16 [4, 8192, 512], P('section', None, 'tp'), may hold values from -0.0625 to 0.0625
- w_out: bfloat16 [4, 4096, 8192], P('section', 'tp'), may hold values from -0.09375 to 0.09375
Outputs:
- layer_out: bfloat16 [4, 2, 128, 8192], P('section', None, 'tp')
- scales_in: float32 [4, 8192], P('section')
- scales_out: float32 [4, 4096], P('section', 'tp')
- smoothed_q: bfloat16 [4, 8192, 4096], P('section', None, 'tp')
- smoothed_k: bfloat16 [4, 8192, 512], P('section', None, 'tp')
- smoothed_v: bfloat16 [4, 8192, 512], P('section', None, 'tp')
All inputs are finite; a program needn't handle non-finite values.
Results may differ from a plain program's by a relative error of at most 0.028.
Values may be sent and summed in bfloat16 or wider, within the bound.
A program may use at most 128 MiB of HBM per device.

v0:
```python
import functools
import math

import jax
import jax.numpy as jnp
from jax import lax
from jax.experimental import pallas as pl
from jax.experimental.pallas import tpu as pltpu
from jax.sharding import PartitionSpec as P

KV_HEADS = 4
HEAD_DIM = 128


norm_eps = 1e-05
stat_eps = 1e-05
rope_base = 500000.0


def rope_tables(length, head_size):
    halves = head_size // 2
    freqs = jnp.exp(-math.log(rope_base) * 2.0 * jnp.arange(halves, dtype=jnp.float32) / head_size)
    angles = jnp.arange(length, dtype=jnp.float32)[:, None] * freqs[None, :]
    return (jnp.cos(angles), jnp.sin(angles))


def smoothing(act_peak, weight_peak, alpha_exp):
    return jnp.exp(
        alpha_exp * jnp.log(act_peak + stat_eps)
        - (1.0 - alpha_exp) * jnp.log(weight_peak + stat_eps)
    )


MESH = pl.DeviceIdType.MESH
CHUNKS = 4
TILE = 512


def remote(src, dst, send, recv, where):
    return pltpu.make_async_remote_copy(
        src_ref=src, dst_ref=dst, send_sem=send, recv_sem=recv, device_id=where, device_id_type=MESH
    )


def grid_of(count):
    minor = 1
    while (2 * minor) * (2 * minor) <= count and count % (2 * minor) == 0:
        minor *= 2
    return (count // minor, minor)


def layers_kernel(
    sections,
    count,
    embedded,
    gain,
    wq_hbm,
    wkv_hbm,
    wo_hbm,
    cos2,
    sin2,
    wpeak_in,
    out,
    act_out,
    head_out,
    wpeak_out,
    wq,
    wkv,
    wo,
    xin,
    ag,
    acc_q,
    acc_kv,
    kvbuf,
    krot,
    vall,
    att,
    part,
    r1,
    s2,
    r2,
    own,
    wpbuf,
    load_sem,
    xin_r,
    xin_s,
    ag_s,
    ag_f,
    ag_r,
    kv_s,
    kv_r,
    r1_s,
    r1_r,
    s2_s,
    r2_r,
    wp_s,
    wp_r,
):
    major, minor = grid_of(count)
    section = lax.axis_index("section")
    me = lax.axis_index("tp")
    a = me // minor
    b = me % minor
    micros, rows, width = embedded.shape
    length = rows * count
    query_cols = wq.shape[1]
    kv_cols = wkv.shape[1] // 2
    heads_here = query_cols // HEAD_DIM
    per_head = HEAD_DIM // kv_cols
    span = width // CHUNKS
    loads = [
        pltpu.make_async_copy(wq_hbm, wq, load_sem.at[0]),
        pltpu.make_async_copy(wkv_hbm, wkv, load_sem.at[1]),
        pltpu.make_async_copy(wo_hbm, wo, load_sem.at[2]),
    ]
    for load in loads:
        load.start()

    def peer(number):
        return (section, number)

    def col_peer(step):
        return lax.rem(a + step + major, major)

    def row_peer(step):
        return lax.rem(b + step + minor, minor)

    barrier = pltpu.get_barrier_semaphore()
    for step in range(1, count):
        pl.semaphore_signal(
            barrier, inc=1, device_id=peer(lax.rem(me + step, count)), device_id_type=MESH
        )

    @pl.when(section > 0)
    def _():
        pl.semaphore_signal(barrier, inc=1, device_id=(section - 1, me), device_id_type=MESH)

    @pl.when(section < sections - 1)
    def _():
        pl.semaphore_signal(barrier, inc=1, device_id=(section + 1, me), device_id_type=MESH)

    before = (section + sections - 1) // sections
    after = (2 * sections - 2 - section) // sections
    pl.semaphore_wait(barrier, count - 1 + before + after)

    act_out[...] = jnp.zeros_like(act_out)
    head_out[...] = jnp.zeros_like(head_out)
    positions = lax.broadcasted_iota(jnp.int32, (length, length), 0)
    keys_at = lax.broadcasted_iota(jnp.int32, (length, length), 1)
    causal = positions >= keys_at

    def weight_copy(step):
        return remote(
            wpeak_in,
            wpbuf.at[me],
            wp_s.at[step - 1],
            wp_r.at[me],
            peer(lax.rem(me + step, count)),
        )

    def rotated(values):
        turned = pltpu.roll(values, HEAD_DIM // 2, 1)
        return (values * cos2[...] + turned * sin2[...]).astype(jnp.bfloat16)

    def tile_at(index):
        return pl.ds(pl.multiple_of(index * TILE, TILE), TILE)

    def micro_step(m, first):
        @pl.when(section == 0)
        def _():
            xin[m] = embedded[m]

        @pl.when(section > 0)
        def _():
            remote(
                xin.at[m], xin.at[m], xin_s.at[0], xin_r.at[m], (section - 1, me)
            ).wait_recv()

        def square(index, total):
            values = xin[m, :, tile_at(index)].astype(jnp.float32)
            return total + jnp.sum(values * values, axis=1, keepdims=True)

        total = lax.fori_loop(
            0, width // TILE, square, jnp.zeros((rows, 1), jnp.float32), unroll=True
        )
        inverse = lax.rsqrt(total / width + norm_eps)
        for index in range(width // TILE):
            cols = pl.ds(index * TILE, TILE)
            values = xin[m, :, cols].astype(jnp.float32)
            ag[m, me, :, cols] = (values * inverse * gain[:, cols]).astype(jnp.bfloat16)

        def column_copy(step):
            return remote(
                ag.at[m, me],
                ag.at[m, me],
                ag_s.at[step - 1],
                ag_r.at[m, me],
                peer(col_peer(step) * minor + b),
            )

        def row_copy(origin, order, step):
            return remote(
                ag.at[m, origin],
                ag.at[m, origin],
                ag_f.at[order, step - 1],
                ag_r.at[m, origin],
                peer(a * minor + row_peer(step)),
            )

        for step in range(1, major):
            column_copy(step).start()
        for step in range(1, minor):
            row_copy(me, 0, step).start()
        for order in range(1, major):
            origin = col_peer(-order) * minor + b
            row_copy(origin, order, 1).wait_recv()
            for step in range(1, minor):
                row_copy(origin, order, step).start()
        for order in range(major):
            for step in range(1, minor):
                origin = col_peer(-order) * minor + row_peer(step)
                row_copy(origin, order, step).wait_recv()

        @pl.when(first)
        def _():
            for load in loads:
                load.wait()
            for step in range(1, count):
                weight_copy(step).start()

        acc_q[...] = jnp.zeros_like(acc_q)
        acc_kv[...] = jnp.zeros_like(acc_kv)

        @pl.loop(0, width // TILE)
        def _(index):
            cols = tile_at(index)
            if rows % 16 == 0:
                normed = ag[m, :, :, cols].reshape(length, TILE)
            else:
                wide = ag[m, :, :, cols].astype(jnp.float32)
                normed = wide.reshape(length, TILE).astype(jnp.bfloat16)
            acc_q[...] += jnp.dot(normed, wq[cols, :], preferred_element_type=jnp.float32)
            acc_kv[...] += jnp.dot(normed, wkv[cols, :], preferred_element_type=jnp.float32)
            peak = jnp.max(jnp.abs(normed.astype(jnp.float32)), axis=0, keepdims=True)
            act_out[:, cols] = jnp.maximum(act_out[:, cols], peak)

        kvbuf[m, me] = acc_kv[...].astype(jnp.bfloat16)

        def kv_copy(step):
            return remote(
                kvbuf.at[m, me],
                kvbuf.at[m, me],
                kv_s.at[step - 1],
                kv_r.at[m, me],
                peer(lax.rem(me + step, count)),
            )

        for step in range(1, count):
            kv_copy(step).start()
        queries = [
            rotated(acc_q[:, head * HEAD_DIM : (head + 1) * HEAD_DIM])
            for head in range(heads_here)
        ]
        for step in range(1, count):
            origin = lax.rem(me - step + count, count)
            remote(
                kvbuf.at[m, origin],
                kvbuf.at[m, origin],
                kv_s.at[step - 1],
                kv_r.at[m, origin],
                peer(origin),
            ).wait_recv()
        for group in range(KV_HEADS):
            blocks = [
                kvbuf[m, group * per_head + piece].astype(jnp.float32) for piece in range(per_head)
            ]
            key = jnp.concatenate([block[:, :kv_cols] for block in blocks], axis=1)
            value = jnp.concatenate([block[:, kv_cols:] for block in blocks], axis=1)
            krot[group] = rotated(key)
            vall[group] = value.astype(jnp.bfloat16)
        for head in range(heads_here):
            if heads_here % KV_HEADS == 0:
                group = head % KV_HEADS
            else:
                group = lax.rem(me * heads_here + head, KV_HEADS)
            scores = lax.dot_general(
                queries[head],
                krot[group],
                (((1,), (1,)), ((), ())),
                preferred_element_type=jnp.float32,
            ) / math.sqrt(HEAD_DIM)
            scores = jnp.where(causal, scores, -1e30)
            weights = jnp.exp(scores - jnp.max(scores, axis=1, keepdims=True))
            probs = (weights / jnp.sum(weights, axis=1, keepdims=True)).astype(jnp.bfloat16)
            mixed = jnp.dot(probs, vall[group], preferred_element_type=jnp.float32)
            mixed = mixed.astype(jnp.bfloat16)
            cols = pl.ds(head * HEAD_DIM, HEAD_DIM)
            att[:, cols] = mixed
            peak = jnp.max(jnp.abs(mixed.astype(jnp.float32)), axis=0, keepdims=True)
            head_out[:, cols] = jnp.maximum(head_out[:, cols], peak)

        orders = list(range(1, major)) + [0]

        def first_copy(chunk, step, order):
            other_b = row_peer(step)
            other_a = col_peer(order)
            return remote(
                part.at[chunk, other_b, other_a],
                r1.at[m, chunk, b, other_a],
                r1_s.at[chunk, step - 1, order],
                r1_r.at[m, chunk, b, other_a],
                peer(a * minor + other_b),
            )

        def second_copy(chunk, order):
            return remote(
                s2.at[chunk, order - 1],
                r2.at[m, chunk, a],
                s2_s.at[chunk, order - 1],
                r2_r.at[m, chunk, a],
                peer(col_peer(order) * minor + b),
            )

        for chunk in range(CHUNKS):

            @pl.loop(0, span // TILE)
            def _(index):
                cols = tile_at(index)
                source = tile_at(index + chunk * (span // TILE))
                product = jnp.dot(att[...], wo[:, source], preferred_element_type=jnp.float32)
                for i in range(major):
                    for j in range(minor):
                        top = (i * minor + j) * rows
                        part[chunk, j, i, :, cols] = product[top : top + rows].astype(jnp.bfloat16)

            for order in orders:
                for step in range(1, minor):
                    first_copy(chunk, step, order).start()
        for chunk in range(CHUNKS):
            for order in orders:
                other_a = col_peer(order)
                for step in range(1, minor):
                    origin = row_peer(step)
                    remote(
                        r1.at[m, chunk, origin, other_a],
                        r1.at[m, chunk, origin, other_a],
                        r1_s.at[chunk, step - 1, order],
                        r1_r.at[m, chunk, origin, other_a],
                        peer(a * minor + origin),
                    ).wait_recv()
                for index in range(span // TILE):
                    cols = pl.ds(index * TILE, TILE)
                    total = part[chunk, b, other_a, :, cols].astype(jnp.float32)
                    for step in range(1, minor):
                        total += r1[m, chunk, row_peer(step), other_a, :, cols].astype(jnp.float32)
                    if order == 0:
                        own[chunk, :, cols] = total
                    else:
                        s2[chunk, order - 1, :, cols] = total.astype(jnp.bfloat16)
                if order != 0:
                    second_copy(chunk, order).start()
        for chunk in range(CHUNKS):
            for order in range(1, major):
                origin = col_peer(-order)
                remote(
                    r2.at[m, chunk, origin],
                    r2.at[m, chunk, origin],
                    s2_s.at[chunk, order - 1],
                    r2_r.at[m, chunk, origin],
                    peer(origin * minor + b),
                ).wait_recv()
            for index in range(span // TILE):
                cols = pl.ds(index * TILE, TILE)
                full = pl.ds(chunk * span + index * TILE, TILE)
                total = own[chunk, :, cols]
                for order in range(1, major):
                    total += r2[m, chunk, col_peer(-order), :, cols].astype(jnp.float32)
                out[m, :, full] = (xin[m, :, full].astype(jnp.float32) + total).astype(jnp.bfloat16)

        def onward():
            return remote(
                out.at[m], xin.at[m], xin_s.at[0], xin_r.at[m], (section + 1, me)
            )

        @pl.when(section < sections - 1)
        def _():
            onward().start()

        for step in range(1, major):
            column_copy(step).wait_send()
        for order in range(major):
            for step in range(1, minor):
                row_copy(col_peer(-order) * minor + b, order, step).wait_send()
        for step in range(1, count):
            kv_copy(step).wait_send()
        for chunk in range(CHUNKS):
            for order in orders:
                for step in range(1, minor):
                    first_copy(chunk, step, order).wait_send()
                if order != 0:
                    second_copy(chunk, order).wait_send()

        @pl.when(section < sections - 1)
        def _():
            onward().wait_send()

    @pl.loop(0, micros)
    def _(m):
        micro_step(m, m == 0)

    peak = wpeak_in[...]
    for step in range(1, count):
        origin = lax.rem(me + step, count)
        remote(
            wpeak_in, wpbuf.at[origin], wp_s.at[step - 1], wp_r.at[origin], peer(origin)
        ).wait_recv()
        peak = jnp.maximum(peak, wpbuf[origin])
    wpeak_out[...] = peak
    for step in range(1, count):
        weight_copy(step).wait_send()


def run_layers(sections, count, embedded, gain, wq, wkv, wo, cos2, sin2, wpeak):
    major, minor = grid_of(count)
    micros, rows, width = embedded.shape
    length = rows * count
    query_cols = wq.shape[1]
    kv_two = wkv.shape[1]
    span = width // CHUNKS
    bf16, f32 = jnp.bfloat16, jnp.float32
    vmem = pl.BlockSpec(memory_space=pltpu.VMEM)
    anywhere = pl.BlockSpec(memory_space=pl.ANY)
    dma = pltpu.SemaphoreType.DMA
    return pl.pallas_call(
        functools.partial(layers_kernel, sections, count),
        out_shape=(
            jax.ShapeDtypeStruct((micros, rows, width), bf16),
            jax.ShapeDtypeStruct((1, width), f32),
            jax.ShapeDtypeStruct((1, query_cols), f32),
            jax.ShapeDtypeStruct(wpeak.shape, f32),
        ),
        in_specs=[vmem, vmem, anywhere, anywhere, anywhere, vmem, vmem, vmem],
        out_specs=(vmem, vmem, vmem, vmem),
        scratch_shapes=[
            pltpu.VMEM(wq.shape, bf16),
            pltpu.VMEM(wkv.shape, bf16),
            pltpu.VMEM(wo.shape, bf16),
            pltpu.VMEM((micros, rows, width), bf16),
            pltpu.VMEM((micros, count, rows, width), bf16),
            pltpu.VMEM((length, query_cols), f32),
            pltpu.VMEM((length, kv_two), f32),
            pltpu.VMEM((micros, count, length, kv_two), bf16),
            pltpu.VMEM((KV_HEADS, length, HEAD_DIM), bf16),
            pltpu.VMEM((KV_HEADS, length, HEAD_DIM), bf16),
            pltpu.VMEM((length, query_cols), bf16),
            pltpu.VMEM((CHUNKS, minor, major, rows, span), bf16),
            pltpu.VMEM((micros, CHUNKS, minor, major, rows, span), bf16),
            pltpu.VMEM((CHUNKS, major - 1, rows, span), bf16),
            pltpu.VMEM((micros, CHUNKS, major, rows, span), bf16),
            pltpu.VMEM((CHUNKS, rows, span), f32),
            pltpu.VMEM((count,) + wpeak.shape, f32),
            dma((3,)),
            dma((micros,)),
            dma((1,)),
            dma((major - 1,)),
            dma((major, minor - 1)),
            dma((micros, count)),
            dma((count - 1,)),
            dma((micros, count)),
            dma((CHUNKS, minor - 1, major)),
            dma((micros, CHUNKS, minor, major)),
            dma((CHUNKS, major - 1)),
            dma((micros, CHUNKS, major)),
            dma((count - 1,)),
            dma((count,)),
        ],
        compiler_params=pltpu.CompilerParams(
            collective_id=0, has_side_effects=True, vmem_limit_bytes=60 * 1024 * 1024
        ),
        name="layers",
    )(embedded, gain, wq, wkv, wo, cos2, sin2, wpeak)


def shards(token_ids, alpha_num, embed_table, norm_gain, w_query, w_key, w_value, w_out):
    tp_count = lax.axis_size("tp")
    section_count = lax.axis_size("section")
    section_index = lax.axis_index("section")
    length = token_ids.shape[1]
    vocab_rows = embed_table.shape[0]
    local_ids = token_ids - section_index * vocab_rows
    inside = (local_ids >= 0) & (local_ids < vocab_rows)
    picked = jnp.take(embed_table, jnp.clip(local_ids, 0, vocab_rows - 1), axis=0)
    picked = jnp.where(inside[:, :, None], picked, jnp.zeros_like(picked))
    summed = lax.psum(picked, "section")
    embedded = lax.all_to_all(summed, "tp", split_axis=1, concat_axis=2, tiled=True)
    w_query, w_key, w_value, w_out = w_query[0], w_key[0], w_value[0], w_out[0]
    w_kv = jnp.concatenate([w_key, w_value], axis=1)
    weight_local = jnp.maximum(
        jnp.max(jnp.abs(w_query), axis=1), jnp.max(jnp.abs(w_kv), axis=1)
    ).astype(jnp.float32)
    out_peak = jnp.max(jnp.abs(w_out), axis=1).astype(jnp.float32)
    cosine, sine = rope_tables(length, HEAD_DIM)
    cos2 = jnp.concatenate([cosine, cosine], axis=1)
    sin2 = jnp.concatenate([-sine, sine], axis=1)
    stored, act_peak, head_peak, weight_peak = run_layers(
        section_count,
        tp_count,
        embedded,
        norm_gain,
        w_query,
        w_kv,
        w_out,
        cos2,
        sin2,
        weight_local.reshape(-1, 128),
    )
    alpha_exp = alpha_num[0].astype(jnp.float32) / 10.0
    scale_in = smoothing(act_peak[0], weight_peak.reshape(-1), alpha_exp)
    scale_out = smoothing(head_peak[0], out_peak, alpha_exp)

    def smoothed(weights):
        return (weights.astype(jnp.float32) * scale_in[:, None]).astype(jnp.bfloat16)

    return (
        stored[None],
        scale_in[None],
        scale_out[None],
        smoothed(w_query)[None],
        smoothed(w_key)[None],
        smoothed(w_value)[None],
    )


def solution(mesh):
    return jax.shard_map(
        shards,
        mesh=mesh,
        in_specs=(
            P(),
            P(),
            P("section", "tp"),
            P("section", None),
            P("section", None, "tp"),
            P("section", None, "tp"),
            P("section", None, "tp"),
            P("section", "tp", None),
        ),
        out_specs=(
            P("section", None, "tp", None),
            P("section", None),
            P("section", "tp"),
            P("section", None, "tp"),
            P("section", None, "tp"),
            P("section", None, "tp"),
        ),
        check_vma=False,
    )
```

profile of v0, /device:TPU:5, one launch (start us, length us, event | category | flops | bytes accessed | tf_op | source)
XLA Modules:
  0.0 411.8 jit_solution(3206438680080512200)
XLA Ops:
  7.2 0.0 all-reduce.2.cloned.1.call-start
  7.2 0.7 fusion.4
  7.9 0.7 compare_and_fusion
  8.6 0.1 copy.20
  8.7 0.1 copy.19
  8.9 9.3 %gather_fusion = bf16[256,1024]{1,0:T(8,128)(2,1)S(1)} fusion(bf16[16384,1024]{1,0:T(8,128)(2,1)} %param.10, s32[1024]{0:T(1024)S(1)} %pad_clamp_fusion), kind=kCustom, calls=%fused_computation | custom fusion | bytes 1049600 | tf_op jit(solution)/shard_map/jit(_take)/gather | solution.py:492
  18.2 1.9 broadcast_select_fusion.1
  20.1 0.0 all-reduce.2.cloned.1.call-update
  20.8 0.0 copy-start
  20.8 5.1 %abs_reduce_fusion = bf16[512]{0:T(512)(128)(2,1)S(1)} fusion(bf16[1,512,8192]{2,1,0:T(8,128)(2,1)} %param.15), kind=kLoop, calls=%fused_computation.2 | loop fusion | flops 8388096 | bytes 8389632 | tf_op jit(solution)/shard_map/reduce_max | solution.py:501
  25.9 2.0 copy.24
  27.9 0.0 copy-done
  28.0 1.8 copy.25
  29.7 4.2 %abs_reduce_fusion.2 = (bf16[8192]{0:T(1024)(128)(2,1)S(1)}, bf16[8192,128]{1,0:T(8,128)(2,1)}) fusion(bf16[8192,64]{1,0:T(8,128)(2,1)} %bitcast.29, bf16[8192,64]{1,0:T(8,128)(2,1)S(1)} %bitcast.28), kind=kLoop, calls=%fused_computation.7 | loop fusion | flops 7331840 | bytes 4210688 | tf_op jit(solution)/shard_map/reduce_max | solution.py:499
  33.9 0.3 fusion.3
  34.2 18.3 %all-reduce.2.cloned.1.call-done = bf16[2,128,1024]{2,0,1:T(2,128)(2,1)} async-done(((bf16[2,128,1024]{2,0,1:T(2,128)(2,1)}), bf16[2,128,1024]{2,0,1:T(2,128)(2,1)}) %all-reduce.2.cloned.1.call-update) | async-done | bytes 524304 | tf_op jit(solution)/shard_map/psum | solution.py:494
  52.6 5.7 %all-to-all-start = ((bf16[2,128,1024]{2,0,1:T(2,128)(2,1)}), bf16[2,128,1024]{2,0,1:T(2,128)(2,1)S(1)}, u32[]{:S(2)}, u32[]{:S(2)}) async-start(bf16[2,128,1024]{2,0,1:T(2,128)(2,1)} %all-reduce.2.cloned.1.call-done), calls=%async_computation | async-start | bytes 1048576 | tf_op jit(solution)/shard_map/all_to_all | solution.py:495
  58.2 0.8 pad_maximum_fusion.1
  59.0 5.3 %abs_reduce_fusion.1 = bf16[8192]{0:T(1024)(128)(2,1)S(1)} fusion(bf16[1,8192,512]{2,1,0:T(8,128)(2,1)} %param.12), kind=kLoop, calls=%fused_computation.3 | loop fusion | flops 8380416 | bytes 8404992 | tf_op jit(solution)/shard_map/reduce_max | solution.py:499
  64.3 0.6 bitcast_convert_fusion.wpeak_in
  64.9 6.7 %all-to-all-done = bf16[2,128,1024]{2,0,1:T(2,128)(2,1)S(1)} async-done(((bf16[2,128,1024]{2,0,1:T(2,128)(2,1)}), bf16[2,128,1024]{2,0,1:T(2,128)(2,1)S(1)}, u32[]{:S(2)}, u32[]{:S(2)}) %all-to-all-start) | async-done | bytes 524320 | tf_op jit(solution)/shard_map/all_to_all | solution.py:495
  71.6 0.1 copy.22
  71.7 0.8 copy.26
  72.5 0.0 copy-start.1
  72.5 319.3 %layers.1 = (bf16[2,16,8192]{2,1,0:T(8,128)(2,1)}, f32[1,8192]{1,0:T(1,128)}, f32[1,512]{1,0:T(1,128)}, f32[64,128]{1,0:T(8,128)}) custom-call(bf16[2,16,8192]{2,1,0:T(8,128)(2,1)} %bitcast.30, f32[1,8192]{1,0:T(1,128)} %gain.1, bf16[8192,512]{1,0:T(8,128)(2,1)} %bitcast.26, bf16[8192,128]{1,0:T(8,128)(2,1)} %get-tuple-element.17.wkv_hbm, ...), custom_call_target="tpu_custom_call" | custom-call | tf_op jit(solution)/shard_map/layers/pallas_call | solution.py:434
  391.8 0.8 log_multiply_fusion.1
  392.6 0.8 fusion.2
  393.4 0.0 copy-done.1
  393.4 1.7 multiply_convert_fusion.1
  395.1 0.0 copy-start.3
  395.1 0.0 copy-start.4
  395.1 0.0 copy-start.2
  395.1 7.7 %multiply_convert_fusion = bf16[1,8192,512]{2,1,0:T(8,128)(2,1)} fusion(bf16[1,8192,512]{2,1,0:T(8,128)(2,1)} %param.12, f32[8192]{0:T(1024)S(1)} %get-tuple-element.14), kind=kLoop, calls=%fused_computation.1 | loop fusion | flops 12582912 | bytes 16809984 | tf_op jit(solution)/shard_map/convert_element_type | solution.py:522
  402.9 0.0 copy-done.3
  402.9 0.7 subtract_exponential_fusion
  403.6 0.0 copy-done.4
  403.6 0.6 subtract_exponential_fusion.1
  404.2 0.0 copy-done.2
  404.2 0.8 copy.31
  (3 shorter events, 0.0 us)
Async XLA Ops:
  7.2 45.4 %all-reduce.2.cloned.1.call-start = ((), (), s32[]{:S(2)}) async-start(), calls=%async_computation.1 | async-start | bytes 1048576 | tf_op jit(solution)/shard_map/psum | solution.py:494
  20.8 7.2 %copy-start = (bf16[1,8192,64]{1,2,0:T(8,128)(2,1)S(1)}, bf16[1,8192,64]{1,2,0:T(8,128)(2,1)}, u32[]{:S(2)}) copy-start(bf16[1,8192,64]{1,2,0:T(8,128)(2,1)} %param.14) | copy-start | bytes 3145732
  52.6 19.0 %all-to-all-start = ((bf16[2,128,1024]{2,0,1:T(2,128)(2,1)}), bf16[2,128,1024]{2,0,1:T(2,128)(2,1)S(1)}, u32[]{:S(2)}, u32[]{:S(2)}) async-start(bf16[2,128,1024]{2,0,1:T(2,128)(2,1)} %all-reduce.2.cloned.1.call-done), calls=%async_computation | async-start | bytes 1048576 | tf_op jit(solution)/shard_map/all_to_all | solution.py:495
  72.5 320.9 %copy-start.1 = (bf16[1,8192,64]{1,2,0:T(8,128)(2,1)S(1)}, bf16[1,8192,64]{1,2,0:T(8,128)(2,1)}, u32[]{:S(2)}) copy-start(bf16[1,8192,64]{1,2,0:T(8,128)(2,1)} %param.13) | copy-start | bytes 3145732
  395.1 7.7 %copy-start.3 = (f32[1,8192]{1,0:T(1,128)S(1)}, f32[1,8192]{1,0:T(1,128)}, u32[]{:S(2)}) copy-start(f32[1,8192]{1,0:T(1,128)} %get-tuple-element.11) | copy-start | bytes 98308
  395.1 8.4 %copy-start.4 = (f32[1,512]{1,0:T(1,128)S(1)}, f32[1,512]{1,0:T(1,128)}, u32[]{:S(2)}) copy-start(f32[1,512]{1,0:T(1,128)} %get-tuple-element.13) | copy-start | bytes 6148
  395.1 9.0 %copy-start.2 = (bf16[2,16,8192]{2,1,0:T(8,128)(2,1)S(1)}, bf16[2,16,8192]{2,1,0:T(8,128)(2,1)}, u32[]{:S(2)}) copy-start(bf16[2,16,8192]{2,1,0:T(8,128)(2,1)} %get-tuple-element.10) | copy-start | bytes 1572868
Sparse Core Ops, SparseCore 0:
  20.2 32.2 all-reduce.1
where the time goes:
time: 412 us
  Pallas kernels  319 us (77%)
  other arithmetic  31.9 us (8%)
  waiting for transfers between devices  25 us (6%)
  local copies, waits for them, and re-layouts  15.2 us (4%)
  between operations  14.8 us (4%)
  starting transfers between devices  5.71 us (1%)
    pallas_call x1, Pallas kernels, run_layers(): pl.pallas_call(functools.partial(layers_kernel, sections, count), out_sha...  319 us
    psum x1, waiting for transfers between devices, shards(): summed = lax.psum(picked, 'section')  18.3 us
    convert_element_type x2, other arithmetic, smoothed(): (weights.astype(jnp.float32) * scale_in[:, None]).astype(jnp.bfloat16)  9.44 us
    gather x1, local copies, waits for them, and re-layouts, shards(): jnp.take(embed_table, jnp.clip(local_ids, 0, vocab_rows - 1), axis=0)  9.33 us
  transfers between devices with their start and end apart: 2, of which 2 were waited for; matrix products, arithmetic and copies ran while one was open for 5% of the time, Pallas kernels for 0%

commit v1 on v0

v1 whole, which is shorter than its diff:
```python
import contextlib
import functools
import math

import jax
import jax.numpy as jnp
from jax import lax
from jax.experimental import pallas as pl
from jax.experimental.pallas import tpu as pltpu
from jax.sharding import PartitionSpec as P

KV_HEADS = 4
HEAD_DIM = 128


norm_eps = 1e-05
stat_eps = 1e-05
rope_base = 500000.0


def rope_tables(length, head_size):
    halves = head_size // 2
    freqs = jnp.exp(-math.log(rope_base) * 2.0 * jnp.arange(halves, dtype=jnp.float32) / head_size)
    angles = jnp.arange(length, dtype=jnp.float32)[:, None] * freqs[None, :]
    return (jnp.cos(angles), jnp.sin(angles))


def smoothing(act_peak, weight_peak, alpha_exp):
    return jnp.exp(
        alpha_exp * jnp.log(act_peak + stat_eps)
        - (1.0 - alpha_exp) * jnp.log(weight_peak + stat_eps)
    )


MESH = pl.DeviceIdType.MESH
TILE = 512
LANES = 128


def scope(name):
    return contextlib.nullcontext()


def remote(src, dst, send, recv, where):
    return pltpu.make_async_remote_copy(
        src_ref=src, dst_ref=dst, send_sem=send, recv_sem=recv, device_id=where, device_id_type=MESH
    )


def grid_of(count):
    minor = 1
    while (2 * minor) * (2 * minor) <= count and count % (2 * minor) == 0:
        minor *= 2
    return (count // minor, minor)


def levels_of(sections):
    distances = []
    while (1 << len(distances)) < sections:
        distances.append(1 << len(distances))
    return distances


def layers_kernel(
    sections,
    count,
    picked,
    gain,
    wq,
    wk,
    wv,
    wo,
    cos2,
    sin2,
    out,
    act_out,
    head_out,
    wpeak_out,
    opeak_out,
    emb,
    emb_acc,
    xall,
    ssq,
    acc_q,
    acc_kv,
    kvbuf,
    krot,
    vall,
    att,
    part,
    r1,
    s2,
    r2,
    own,
    wpeak,
    wpbuf,
    emb_s,
    emb_r,
    col_s,
    fwd_s,
    on_s,
    ag_r,
    kv_s,
    kv_r,
    r1_s,
    r1_r,
    s2_s,
    r2_r,
    wp_s,
    wp_r,
):
    major, minor = grid_of(count)
    section = lax.axis_index("section")
    me = lax.axis_index("tp")
    a = me // minor
    b = me % minor
    micros, _, rows, feats = picked.shape
    width = feats * count
    length = rows * count
    query_cols = wq.shape[1]
    kv_cols = wk.shape[0]
    heads_here = query_cols // HEAD_DIM
    per_head = HEAD_DIM // kv_cols
    chunks = major
    span = width // chunks
    distances = levels_of(sections)
    later = (section + sections - 1) // sections

    def peer(number):
        return (section, number)

    def col_peer(step):
        return lax.rem(a + step + major, major)

    def row_peer(step):
        return lax.rem(b + step + minor, minor)

    with scope("p_barrier"):
        barrier = pltpu.get_barrier_semaphore()
        for step in range(1, count):
            pl.semaphore_signal(
                barrier, inc=1, device_id=peer(lax.rem(me + step, count)), device_id_type=MESH
            )

        @pl.when(section > 0)
        def _():
            for step in range(major):
                pl.semaphore_signal(
                    barrier,
                    inc=1,
                    device_id=(section - 1, col_peer(step) * minor + b),
                    device_id_type=MESH,
                )

        @pl.when(section < sections - 1)
        def _():
            for step in range(major):
                pl.semaphore_signal(
                    barrier,
                    inc=1,
                    device_id=(section + 1, col_peer(step) * minor + b),
                    device_id_type=MESH,
                )

        expected = count - 1 + major * later + major * ((2 * sections - 2 - section) // sections)
        for distance in distances[1:]:
            partner = section + distance * (1 - 2 * ((section // distance) % 2))

            @pl.when(section % distance == 0)
            def _():
                pl.semaphore_signal(barrier, inc=1, device_id=(partner, me), device_id_type=MESH)

            expected += 1 - (section % distance + distance - 1) // distance
        pl.semaphore_wait(barrier, expected)

    def embed_copy(m, level):
        distance = distances[level]
        source = picked if level == 0 else emb_acc
        return remote(
            source.at[m],
            emb.at[level, m],
            emb_s.at[level, m],
            emb_r.at[level, m],
            (section - distance, me),
        )

    def embed_arrival(m, level):
        return remote(
            emb.at[level, m],
            emb.at[level, m],
            emb_s.at[level, m],
            emb_r.at[level, m],
            (section + distances[level], me),
        )

    def embed_tree(m):
        for level, distance in enumerate(distances):

            @pl.when(section % (2 * distance) == distance)
            def _():
                embed_copy(m, level).start()

            if level < len(distances) - 1:

                @pl.when(section % (2 * distance) == 0)
                def _():
                    embed_arrival(m, level).wait_recv()
                    source = picked if level == 0 else emb_acc
                    emb_acc[m] = source[m] + emb[level, m]

    def first_piece(m, chunk, side, sub):
        return xall.at[
            m, chunk, pl.ds(sub * minor, minor), :, pl.ds(pl.multiple_of(side * feats, feats), feats)
        ]

    def first_column(m, sub, step):
        piece = first_piece(m, a, b, sub)
        return remote(
            piece,
            piece,
            col_s.at[m, sub, step - 1],
            ag_r.at[m, a, sub * minor + b],
            peer(col_peer(step) * minor + b),
        )

    def first_forward(m, order, sub, step):
        chunk = col_peer(-order)
        piece = first_piece(m, chunk, b, sub)
        return remote(
            piece,
            piece,
            fwd_s.at[m, order, sub, step - 1],
            ag_r.at[m, chunk, sub * minor + b],
            peer(a * minor + row_peer(step)),
        )

    def embed_finish(m):
        level = len(distances) - 1
        embed_arrival(m, level).wait_recv()
        source = picked if level == 0 else emb_acc
        cols = pl.ds(pl.multiple_of(b * feats, feats), feats)
        xall[m, a, :, :, cols] = source[m] + emb[level, m]
        for sub in range(major):
            for step in range(1, minor):
                first_forward(m, 0, sub, step).start()
            for step in range(1, major):
                first_column(m, sub, step).start()

    @pl.when(section > 0)
    def _():
        for m in range(micros):
            embed_tree(m)

    with scope("p_wpeak"):
        act_out[...] = jnp.zeros_like(act_out)
        head_out[...] = jnp.zeros_like(head_out)
        positions = lax.broadcasted_iota(jnp.int32, (length, length), 0)
        keys_at = lax.broadcasted_iota(jnp.int32, (length, length), 1)
        causal = positions >= keys_at

        @pl.loop(0, width // LANES)
        def _(index):
            span_rows = pl.ds(pl.multiple_of(index * LANES, LANES), LANES)
            block = jnp.abs(wq[span_rows, :])
            peak = block[:, :LANES]
            for piece in range(1, query_cols // LANES):
                peak = jnp.maximum(peak, block[:, piece * LANES : (piece + 1) * LANES])
            turned = jnp.max(peak.astype(jnp.float32).T, axis=0, keepdims=True)
            keys = jnp.max(jnp.abs(wk[:, span_rows]).astype(jnp.float32), axis=0, keepdims=True)
            values = jnp.max(jnp.abs(wv[:, span_rows]).astype(jnp.float32), axis=0, keepdims=True)
            wpeak[:, span_rows] = jnp.maximum(turned, jnp.maximum(keys, values))

        for piece in range(query_cols // LANES):
            span_rows = pl.ds(piece * LANES, LANES)

            def widest(index, peak):
                cols = pl.ds(pl.multiple_of(index * TILE, TILE), TILE)
                block = jnp.abs(wo[span_rows, cols])
                for inner in range(TILE // LANES):
                    peak = jnp.maximum(peak, block[:, inner * LANES : (inner + 1) * LANES])
                return peak

            peak = lax.fori_loop(
                0, width // TILE, widest, jnp.zeros((LANES, LANES), jnp.bfloat16)
            )
            opeak_out[:, span_rows] = jnp.max(peak.astype(jnp.float32).T, axis=0, keepdims=True)

    @pl.when(section == 0)
    def _():
        embed_tree(0)
        embed_finish(0)
        for m in range(1, micros):
            embed_tree(m)

    def weight_copy(step):
        return remote(
            wpeak,
            wpbuf.at[me],
            wp_s.at[step - 1],
            wp_r.at[me],
            peer(lax.rem(me + step, count)),
        )

    def rotated(values):
        turned = pltpu.roll(values, HEAD_DIM // 2, 1)
        return (values * cos2[...] + turned * sin2[...]).astype(jnp.bfloat16)

    def tile_at(index):
        return pl.ds(pl.multiple_of(index * TILE, TILE), TILE)

    def forward(m, chunk, order, step):
        origin = col_peer(-order) * minor + b
        return remote(
            xall.at[m, chunk, origin],
            xall.at[m, chunk, origin],
            fwd_s.at[m, chunk, order, step - 1],
            ag_r.at[m, chunk, origin],
            peer(a * minor + row_peer(step)),
        )

    def onward(m, chunk, step):
        return remote(
            out.at[m, :, pl.ds(chunk * span, span)],
            xall.at[m, chunk, me],
            on_s.at[m, chunk, step],
            ag_r.at[m, chunk, me],
            (section + 1, col_peer(step) * minor + b),
        )

    def kv_copy(m, step):
        return remote(
            kvbuf.at[m, me],
            kvbuf.at[m, me],
            kv_s.at[m, step - 1],
            kv_r.at[m, me],
            peer(lax.rem(me + step, count)),
        )

    orders = list(range(1, major)) + [0]

    def first_copy(m, chunk, step, order):
        other_b = row_peer(step)
        other_a = col_peer(order)
        return remote(
            part.at[m, chunk, other_b, other_a],
            r1.at[m, chunk, b, other_a],
            r1_s.at[m, chunk, step - 1, order],
            r1_r.at[m, chunk, b, other_a],
            peer(a * minor + other_b),
        )

    def second_copy(m, chunk, order):
        return remote(
            s2.at[m, chunk, order - 1],
            r2.at[m, chunk, a],
            s2_s.at[m, chunk, order - 1],
            r2_r.at[m, chunk, a],
            peer(col_peer(order) * minor + b),
        )

    def micro_step(m):
        acc_q[...] = jnp.zeros_like(acc_q)
        acc_kv[...] = jnp.zeros_like(acc_kv)
        ssq[...] = jnp.zeros_like(ssq)

        def consume(chunk):
            @pl.loop(0, span // TILE)
            def _(index):
                cols = tile_at(index)
                full = pl.ds(pl.multiple_of(chunk * span + index * TILE, TILE), TILE)
                values = xall[m, chunk, :, :, cols].astype(jnp.float32).reshape(length, TILE)
                square = values * values
                total = square[:, :LANES]
                for piece in range(1, TILE // LANES):
                    total += square[:, piece * LANES : (piece + 1) * LANES]
                ssq[...] += total
                gained = (values * gain[:, full]).astype(jnp.bfloat16)
                acc_q[...] += jnp.dot(gained, wq[full, :], preferred_element_type=jnp.float32)
                wkv = jnp.concatenate([wk[:, full], wv[:, full]], axis=0)
                acc_kv[...] += lax.dot_general(
                    gained, wkv, (((1,), (1,)), ((), ())), preferred_element_type=jnp.float32
                )

        for turn in range(chunks + 1):
            if turn < chunks:
                with scope(f"p_col{turn}"):
                    if turn > 0:

                        @pl.when(section == 0)
                        def _():
                            chunk = col_peer(-turn)
                            for sub in range(major):
                                piece = first_piece(m, chunk, b, sub)
                                remote(
                                    piece,
                                    piece,
                                    fwd_s.at[m, turn, sub, 0],
                                    ag_r.at[m, chunk, sub * minor + b],
                                    peer(chunk * minor + b),
                                ).wait_recv()
                                for step in range(1, minor):
                                    first_forward(m, turn, sub, step).start()

                    @pl.when(section > 0)
                    def _():
                        for order in range(major):
                            origin = col_peer(-order) * minor + b
                            remote(
                                xall.at[m, turn, origin],
                                xall.at[m, turn, origin],
                                fwd_s.at[m, turn, order, 0],
                                ag_r.at[m, turn, origin],
                                (section - 1, origin),
                            ).wait_recv()
                            for step in range(1, minor):
                                forward(m, turn, order, step).start()

            if turn > 0:
                done = turn - 1
                with scope(f"p_row{done}"):

                    @pl.when(section == 0)
                    def _():
                        chunk = col_peer(-done)
                        for sub in range(major):
                            for step in range(1, minor):
                                side = row_peer(step)
                                piece = first_piece(m, chunk, side, sub)
                                remote(
                                    piece,
                                    piece,
                                    fwd_s.at[m, done, sub, step - 1],
                                    ag_r.at[m, chunk, sub * minor + side],
                                    peer(a * minor + side),
                                ).wait_recv()

                    @pl.when(section > 0)
                    def _():
                        for order in range(major):
                            for step in range(1, minor):
                                side = row_peer(step)
                                origin = col_peer(-order) * minor + side
                                remote(
                                    xall.at[m, done, origin],
                                    xall.at[m, done, origin],
                                    fwd_s.at[m, done, order, step - 1],
                                    ag_r.at[m, done, origin],
                                    peer(a * minor + side),
                                ).wait_recv()

                with scope(f"p_qkv{done}"):
                    consume(done * later + (1 - later) * col_peer(-done))

        with scope("p_scale"):
            inverse = lax.rsqrt(jnp.sum(ssq[...], axis=1, keepdims=True) / width + norm_eps)
            kvbuf[m, me] = (acc_kv[...] * inverse).astype(jnp.bfloat16)
            for step in range(1, count):
                kv_copy(m, step).start()

            @pl.when(jnp.logical_and(section == 0, m < micros - 1))
            def _():
                embed_finish(m + 1)

            queries = [
                rotated(acc_q[:, head * HEAD_DIM : (head + 1) * HEAD_DIM] * inverse)
                for head in range(heads_here)
            ]

        with scope("p_actpeak"):
            for chunk in range(chunks):

                @pl.loop(0, span // TILE)
                def _(index):
                    cols = tile_at(index)
                    full = pl.ds(pl.multiple_of(chunk * span + index * TILE, TILE), TILE)
                    values = xall[m, chunk, :, :, cols].astype(jnp.float32).reshape(length, TILE)
                    peak = jnp.max(jnp.abs(values * inverse), axis=0, keepdims=True)
                    peak = (peak * jnp.abs(gain[:, full])).astype(jnp.bfloat16)
                    act_out[:, full] = jnp.maximum(act_out[:, full], peak.astype(jnp.float32))

        with scope("p_kvwait"):
            for step in range(1, count):
                origin = lax.rem(me - step + count, count)
                remote(
                    kvbuf.at[m, origin],
                    kvbuf.at[m, origin],
                    kv_s.at[m, step - 1],
                    kv_r.at[m, origin],
                    peer(origin),
                ).wait_recv()
        with scope("p_attn"):
            for group in range(KV_HEADS):
                blocks = [
                    kvbuf[m, group * per_head + piece].astype(jnp.float32)
                    for piece in range(per_head)
                ]
                key = jnp.concatenate([block[:, :kv_cols] for block in blocks], axis=1)
                value = jnp.concatenate([block[:, kv_cols:] for block in blocks], axis=1)
                krot[group] = rotated(key)
                vall[group] = value.astype(jnp.bfloat16)
            for head in range(heads_here):
                if heads_here % KV_HEADS == 0:
                    group = head % KV_HEADS
                else:
                    group = lax.rem(me * heads_here + head, KV_HEADS)
                scores = lax.dot_general(
                    queries[head],
                    krot[group],
                    (((1,), (1,)), ((), ())),
                    preferred_element_type=jnp.float32,
                ) / math.sqrt(HEAD_DIM)
                scores = jnp.where(causal, scores, -1e30)
                weights = jnp.exp(scores - jnp.max(scores, axis=1, keepdims=True))
                probs = (weights / jnp.sum(weights, axis=1, keepdims=True)).astype(jnp.bfloat16)
                mixed = jnp.dot(probs, vall[group], preferred_element_type=jnp.float32)
                mixed = mixed.astype(jnp.bfloat16)
                cols = pl.ds(head * HEAD_DIM, HEAD_DIM)
                att[:, cols] = mixed
                peak = jnp.max(jnp.abs(mixed.astype(jnp.float32)), axis=0, keepdims=True)
                head_out[:, cols] = jnp.maximum(head_out[:, cols], peak)

        with scope("p_oproj"):
            for chunk in range(chunks):

                @pl.loop(0, span // TILE)
                def _(index):
                    cols = tile_at(index)
                    source = tile_at(index + chunk * (span // TILE))
                    product = jnp.dot(att[...], wo[:, source], preferred_element_type=jnp.float32)
                    for i in range(major):
                        for j in range(minor):
                            top = (i * minor + j) * rows
                            part[m, chunk, j, i, :, cols] = product[top : top + rows].astype(
                                jnp.bfloat16
                            )

                for order in orders:
                    for step in range(1, minor):
                        first_copy(m, chunk, step, order).start()

        def first_sum(chunk):
            for order in orders:
                other_a = col_peer(order)
                for step in range(1, minor):
                    origin = row_peer(step)
                    remote(
                        r1.at[m, chunk, origin, other_a],
                        r1.at[m, chunk, origin, other_a],
                        r1_s.at[m, chunk, step - 1, order],
                        r1_r.at[m, chunk, origin, other_a],
                        peer(a * minor + origin),
                    ).wait_recv()
                for index in range(span // TILE):
                    cols = pl.ds(index * TILE, TILE)
                    total = part[m, chunk, b, other_a, :, cols].astype(jnp.float32)
                    for step in range(1, minor):
                        total += r1[m, chunk, row_peer(step), other_a, :, cols].astype(jnp.float32)
                    if order == 0:
                        own[chunk, :, cols] = total
                    else:
                        s2[m, chunk, order - 1, :, cols] = total.astype(jnp.bfloat16)
                if order != 0:
                    second_copy(m, chunk, order).start()

        def second_sum(chunk):
            for order in range(1, major):
                origin = col_peer(-order)
                remote(
                    r2.at[m, chunk, origin],
                    r2.at[m, chunk, origin],
                    s2_s.at[m, chunk, order - 1],
                    r2_r.at[m, chunk, origin],
                    peer(origin * minor + b),
                ).wait_recv()
            for index in range(span // TILE):
                cols = pl.ds(index * TILE, TILE)
                full = pl.ds(chunk * span + index * TILE, TILE)
                total = own[chunk, :, cols]
                for order in range(1, major):
                    total += r2[m, chunk, col_peer(-order), :, cols].astype(jnp.float32)
                rest = xall[m, chunk, me, :, cols].astype(jnp.float32)
                out[m, :, full] = (rest + total).astype(jnp.bfloat16)

            @pl.when(section < sections - 1)
            def _():
                for step in range(major):
                    onward(m, chunk, step).start()

        for chunk in range(chunks + 1):
            if chunk < chunks:
                with scope(f"p_rs1_{chunk}"):
                    first_sum(chunk)
            if chunk > 0:
                with scope(f"p_rs2_{chunk - 1}"):
                    second_sum(chunk - 1)

        @pl.when(m == 0)
        def _():
            for step in range(1, count):
                weight_copy(step).start()

    @pl.loop(0, micros)
    def _(m):
        micro_step(m)

    with scope("p_wpwait"):
        peak = wpeak[...]
        for step in range(1, count):
            origin = lax.rem(me + step, count)
            remote(
                wpeak, wpbuf.at[origin], wp_s.at[step - 1], wp_r.at[origin], peer(origin)
            ).wait_recv()
            peak = jnp.maximum(peak, wpbuf[origin])
        wpeak_out[...] = peak

    with scope("p_sends"):
        for level, distance in enumerate(distances):

            @pl.when(section % (2 * distance) == distance)
            def _():
                for m in range(micros):
                    embed_copy(m, level).wait_send()

        for m in range(micros):

            @pl.when(section == 0)
            def _():
                for sub in range(major):
                    for step in range(1, major):
                        first_column(m, sub, step).wait_send()
                for order in range(major):
                    for sub in range(major):
                        for step in range(1, minor):
                            first_forward(m, order, sub, step).wait_send()

            @pl.when(section > 0)
            def _():
                for chunk in range(chunks):
                    for order in range(major):
                        for step in range(1, minor):
                            forward(m, chunk, order, step).wait_send()

            @pl.when(section < sections - 1)
            def _():
                for chunk in range(chunks):
                    for step in range(major):
                        onward(m, chunk, step).wait_send()

            for step in range(1, count):
                kv_copy(m, step).wait_send()
            for chunk in range(chunks):
                for order in orders:
                    for step in range(1, minor):
                        first_copy(m, chunk, step, order).wait_send()
                    if order != 0:
                        second_copy(m, chunk, order).wait_send()
        for step in range(1, count):
            weight_copy(step).wait_send()


def run_layers(sections, count, picked, gain, wq, wk, wv, wo, cos2, sin2):
    major, minor = grid_of(count)
    micros, _, rows, feats = picked.shape
    width = feats * count
    length = rows * count
    query_cols = wq.shape[1]
    kv_two = 2 * wk.shape[0]
    levels = len(levels_of(sections))
    chunks = major
    span = width // chunks
    bf16, f32 = jnp.bfloat16, jnp.float32
    vmem = pl.BlockSpec(memory_space=pltpu.VMEM)
    dma = pltpu.SemaphoreType.DMA
    return pl.pallas_call(
        functools.partial(layers_kernel, sections, count),
        out_shape=(
            jax.ShapeDtypeStruct((micros, rows, width), bf16),
            jax.ShapeDtypeStruct((1, width), f32),
            jax.ShapeDtypeStruct((1, query_cols), f32),
            jax.ShapeDtypeStruct((1, width), f32),
            jax.ShapeDtypeStruct((1, query_cols), f32),
        ),
        in_specs=[vmem] * 8,
        out_specs=(vmem,) * 5,
        scratch_shapes=[
            pltpu.VMEM((levels, micros, count, rows, feats), bf16),
            pltpu.VMEM((micros, count, rows, feats), bf16),
            pltpu.VMEM((micros, chunks, count, rows, span), bf16),
            pltpu.VMEM((length, LANES), f32),
            pltpu.VMEM((length, query_cols), f32),
            pltpu.VMEM((length, kv_two), f32),
            pltpu.VMEM((micros, count, length, kv_two), bf16),
            pltpu.VMEM((KV_HEADS, length, HEAD_DIM), bf16),
            pltpu.VMEM((KV_HEADS, length, HEAD_DIM), bf16),
            pltpu.VMEM((length, query_cols), bf16),
            pltpu.VMEM((micros, chunks, minor, major, rows, span), bf16),
            pltpu.VMEM((micros, chunks, minor, major, rows, span), bf16),
            pltpu.VMEM((micros, chunks, major - 1, rows, span), bf16),
            pltpu.VMEM((micros, chunks, major, rows, span), bf16),
            pltpu.VMEM((chunks, rows, span), f32),
            pltpu.VMEM((1, width), f32),
            pltpu.VMEM((count, 1, width), f32),
            dma((levels, micros)),
            dma((levels, micros)),
            dma((micros, major, major - 1)),
            dma((micros, chunks, major, minor - 1)),
            dma((micros, chunks, major)),
            dma((micros, chunks, count)),
            dma((micros, count - 1)),
            dma((micros, count)),
            dma((micros, chunks, minor - 1, major)),
            dma((micros, chunks, minor, major)),
            dma((micros, chunks, major - 1)),
            dma((micros, chunks, major)),
            dma((count - 1,)),
            dma((count,)),
        ],
        compiler_params=pltpu.CompilerParams(
            collective_id=0, has_side_effects=True, vmem_limit_bytes=VMEM_MIB * 1024 * 1024
        ),
        name="layers",
    )(picked, gain, wq, wk, wv, wo, cos2, sin2)


VMEM_MIB = 24


def shards(token_ids, alpha_num, embed_table, norm_gain, w_query, w_key, w_value, w_out):
    tp_count = lax.axis_size("tp")
    section_count = lax.axis_size("section")
    section_index = lax.axis_index("section")
    micros, length = token_ids.shape
    vocab_rows, feats = embed_table.shape
    local_ids = token_ids - section_index * vocab_rows
    inside = (local_ids >= 0) & (local_ids < vocab_rows)
    picked = jnp.take(embed_table, jnp.clip(local_ids, 0, vocab_rows - 1), axis=0)
    picked = jnp.where(inside[:, :, None], picked, jnp.zeros_like(picked))
    picked = picked.reshape(micros, tp_count, length // tp_count, feats)
    w_query, w_key, w_value, w_out = w_query[0], w_key[0], w_value[0], w_out[0]
    cosine, sine = rope_tables(length, HEAD_DIM)
    cos2 = jnp.concatenate([cosine, cosine], axis=1)
    sin2 = jnp.concatenate([-sine, sine], axis=1)
    stored, act_peak, head_peak, weight_peak, out_peak = run_layers(
        section_count,
        tp_count,
        picked,
        norm_gain,
        w_query,
        w_key.T,
        w_value.T,
        w_out,
        cos2,
        sin2,
    )
    alpha_exp = alpha_num[0].astype(jnp.float32) / 10.0
    scale_in = smoothing(act_peak[0], weight_peak[0], alpha_exp)
    scale_out = smoothing(head_peak[0], out_peak[0], alpha_exp)

    def smoothed(weights):
        return (weights.astype(jnp.float32) * scale_in[:, None]).astype(jnp.bfloat16)

    return (
        stored[None],
        scale_in[None],
        scale_out[None],
        smoothed(w_query)[None],
        smoothed(w_key)[None],
        smoothed(w_value)[None],
    )


def solution(mesh):
    return jax.shard_map(
        shards,
        mesh=mesh,
        in_specs=(
            P(),
            P(),
            P("section", "tp"),
            P("section", None),
            P("section", None, "tp"),
            P("section", None, "tp"),
            P("section", None, "tp"),
            P("section", "tp", None),
        ),
        out_specs=(
            P("section", None, "tp", None),
            P("section", None),
            P("section", "tp"),
            P("section", None, "tp"),
            P("section", None, "tp"),
            P("section", None, "tp"),
        ),
        check_vma=False,
    )
```

time: 412 us -> 306 us (0.74)
  Pallas kernels: 319 us -> 276 us
  waiting for transfers between devices: 25 us -> 0 us
  other arithmetic: 31.9 us -> 8.57 us
  between operations: 14.8 us -> 1.35 us
  starting transfers between devices: 5.71 us -> 0 us
  local copies, waits for them, and re-layouts: 15.2 us -> 20.2 us
    pallas_call x1, Pallas kernels: 319 us -> 276 us  [run_layers(): pl.pallas_call(functools.partial(layers_kernel, sections, count), out_sha...]
    psum x1 -> x0, waiting for transfers between devices: 18.3 us -> none  [shards(): summed = lax.psum(picked, 'section')]
    reduce_max x3 -> x0, other arithmetic: 14.6 us -> none  [the longest x1 5.3 us: shards(): jnp.max(jnp.abs(w_query), axis=1)]
    all_to_all x1 -> x0, waiting for transfers between devices: 6.66 us -> none  [shards(): lax.all_to_all(summed, 'tp', split_axis=1, concat_axis=2, tiled=True)]
    unnamed x13, local copies, waits for them, and re-layouts: 4.61 us -> 10.8 us
    all_to_all x1 -> x0, starting transfers between devices: 5.68 us -> none  [shards(): lax.all_to_all(summed, 'tp', split_axis=1, concat_axis=2, tiled=True)]
  transfers between devices with their start and end apart: 2 -> 0, of which waited for: 2 -> 0; matrix products, arithmetic and copies ran while one was open for 5% -> 0% of each run, Pallas kernels for 0% -> 0%
where the time goes in v1:
time: 306 us
  Pallas kernels  276 us (90%)
  local copies, waits for them, and re-layouts  20.2 us (7%)
  other arithmetic  8.57 us (3%)
    pallas_call x1, Pallas kernels, run_layers(): pl.pallas_call(functools.partial(layers_kernel, sections, count), out_sha...  276 us
    unnamed x13, local copies, waits for them, and re-layouts  10.8 us
    gather x1, local copies, waits for them, and re-layouts, shards(): jnp.take(embed_table, jnp.clip(local_ids, 0, vocab_rows - 1), axis=0)  9.24 us

profile of v1, /device:TPU:5, one launch (start us, length us, event | category | flops | bytes accessed | tf_op | source)
XLA Modules:
  0.0 306.0 jit_solution(5266817240012230077)
XLA Ops:
  1.3 0.7 fusion.3
  2.0 0.7 compare_and_fusion.1
  2.7 0.1 broadcast_in_dim.41
  2.8 0.1 broadcast_in_dim.43
  2.9 0.3 fusion.2
  3.1 0.1 pad_maximum_fusion
  3.2 9.2 %gather_fusion = bf16[256,1024]{1,0:T(8,128)(2,1)S(1)} fusion(bf16[16384,1024]{1,0:T(8,128)(2,1)} %param.10, s32[1024]{0:T(1024)S(1)} %pad_clamp_fusion), kind=kCustom, calls=%fused_computation | custom fusion | bytes 1049600 | tf_op jit(solution)/shard_map/jit(_take)/gather | solution.py:736
  12.5 0.1 select_select_fusion.picked
  12.6 0.0 copy-start
  12.6 3.4 %copy-done = bf16[1,8192,512]{2,1,0:T(8,128)(2,1)S(1)} copy-done((bf16[1,8192,512]{2,1,0:T(8,128)(2,1)S(1)}, bf16[1,8192,512]{2,1,0:T(8,128)(2,1)}, u32[]{:S(2)}) %copy-start) | copy-done | bytes 8388632
  16.0 0.0 copy-start.1
  16.0 3.4 %copy-done.1 = bf16[1,512,8192]{2,1,0:T(8,128)(2,1)S(1)} copy-done((bf16[1,512,8192]{2,1,0:T(8,128)(2,1)S(1)}, bf16[1,512,8192]{2,1,0:T(8,128)(2,1)}, u32[]{:S(2)}) %copy-start.1) | copy-done | bytes 8388632
  19.4 0.0 copy-start.2
  19.4 1.2 copy-done.2
  20.6 0.0 copy-start.3
  20.6 1.2 copy-done.3
  21.8 0.0 copy-start.4
  21.8 0.8 copy-done.4
  22.6 275.9 %layers.1 = (bf16[2,16,8192]{2,1,0:T(8,128)(2,1)S(1)}, f32[1,8192]{1,0:T(1,128)S(1)}, f32[1,512]{1,0:T(1,128)S(1)}, f32[1,8192]{1,0:T(1,128)S(1)}, f32[1,512]{1,0:T(1,128)S(1)}) custom-call(bf16[2,8,16,1024]{3,2,1,0:T(8,128)(2,1)S(1)} %select_select_fusion.picked, f32[1,8192]{1,0:T(1,128)S(1)} %copy-done.4, bf16[8192,512]{1,0:T(8,128)(2,1)S(1)} %bitcast.14, ...), custom_call_target="tpu_custom_call" | custom-call | tf_op jit(solution)/shard_map/layers/pallas_call | solution.py:674
  298.5 0.6 subtract_exponential_fusion.1
  299.1 0.1 subtract_exponential_fusion
  299.2 0.0 copy-start.5
  299.3 1.7 multiply_convert_fusion.1
  301.0 4.2 %multiply_convert_fusion = bf16[1,8192,512]{2,1,0:T(8,128)(2,1)} fusion(bf16[1,8192,512]{2,1,0:T(8,128)(2,1)S(1)} %copy-done, f32[8192]{0:T(1024)S(1)} %bitcast.21), kind=kLoop, calls=%fused_computation.1 | loop fusion | flops 12582912 | bytes 16809984 | tf_op jit(solution)/shard_map/convert_element_type | solution.py:760
  305.2 0.0 copy-done.5
  305.2 0.8 copy.16
  (2 shorter events, 0.0 us)
Async XLA Ops:
  12.6 3.4 %copy-start = (bf16[1,8192,512]{2,1,0:T(8,128)(2,1)S(1)}, bf16[1,8192,512]{2,1,0:T(8,128)(2,1)}, u32[]{:S(2)}) copy-start(bf16[1,8192,512]{2,1,0:T(8,128)(2,1)} %param.12) | copy-start | bytes 25165828
  16.0 3.4 %copy-start.1 = (bf16[1,512,8192]{2,1,0:T(8,128)(2,1)S(1)}, bf16[1,512,8192]{2,1,0:T(8,128)(2,1)}, u32[]{:S(2)}) copy-start(bf16[1,512,8192]{2,1,0:T(8,128)(2,1)} %param.15) | copy-start | bytes 25165828
  19.4 1.2 copy-start.2
  20.6 1.2 copy-start.3
  21.8 0.8 copy-start.4
  299.2 6.0 %copy-start.5 = (f32[1,8192]{1,0:T(1,128)}, f32[1,8192]{1,0:T(1,128)S(1)}, u32[]{:S(2)}) copy-start(f32[1,8192]{1,0:T(1,128)S(1)} %subtract_exponential_fusion) | copy-start | bytes 98308

commit v2 on v1

--- a/solution.py
+++ b/solution.py
@@ -66,17 +66,24 @@
     count,
     picked,
     gain,
+    wq_hbm,
+    wk_hbm,
+    wv_hbm,
+    wo_hbm,
+    cos2,
+    sin2,
+    alpha,
+    out,
+    scale_in,
+    scale_out,
     wq,
     wk,
     wv,
     wo,
-    cos2,
-    sin2,
-    out,
-    act_out,
-    head_out,
-    wpeak_out,
-    opeak_out,
+    act_peak,
+    head_peak,
+    opeak,
+    qrot,
     emb,
     emb_acc,
     xall,
@@ -94,6 +101,7 @@
     own,
     wpeak,
     wpbuf,
+    load_sem,
     emb_s,
     emb_r,
     col_s,
@@ -108,6 +116,7 @@
     r2_r,
     wp_s,
     wp_r,
+    gate,
 ):
     major, minor = grid_of(count)
     section = lax.axis_index("section")
@@ -135,6 +144,15 @@
     def row_peer(step):
         return lax.rem(b + step + minor, minor)
 
+    loads = [
+        pltpu.make_async_copy(wq_hbm, wq, load_sem.at[0]),
+        pltpu.make_async_copy(wk_hbm, wk, load_sem.at[1]),
+        pltpu.make_async_copy(wv_hbm, wv, load_sem.at[2]),
+        pltpu.make_async_copy(wo_hbm, wo, load_sem.at[3]),
+    ]
+    for load in loads:
+        load.start()
+
     with scope("p_barrier"):
         barrier = pltpu.get_barrier_semaphore()
         for step in range(1, count):
@@ -246,18 +264,13 @@
             for step in range(1, major):
                 first_column(m, sub, step).start()
 
-    @pl.when(section > 0)
-    def _():
-        for m in range(micros):
-            embed_tree(m)
-
-    with scope("p_wpeak"):
-        act_out[...] = jnp.zeros_like(act_out)
-        head_out[...] = jnp.zeros_like(head_out)
-        positions = lax.broadcasted_iota(jnp.int32, (length, length), 0)
-        keys_at = lax.broadcasted_iota(jnp.int32, (length, length), 1)
-        causal = positions >= keys_at
-
+    act_peak[...] = jnp.zeros_like(act_peak)
+    head_peak[...] = jnp.zeros_like(head_peak)
+    positions = lax.broadcasted_iota(jnp.int32, (length, length), 0)
+    keys_at = lax.broadcasted_iota(jnp.int32, (length, length), 1)
+    causal = positions >= keys_at
+
+    def weight_peaks():
         @pl.loop(0, width // LANES)
         def _(index):
             span_rows = pl.ds(pl.multiple_of(index * LANES, LANES), LANES)
@@ -283,14 +296,31 @@
             peak = lax.fori_loop(
                 0, width // TILE, widest, jnp.zeros((LANES, LANES), jnp.bfloat16)
             )
-            opeak_out[:, span_rows] = jnp.max(peak.astype(jnp.float32).T, axis=0, keepdims=True)
-
-    @pl.when(section == 0)
-    def _():
-        embed_tree(0)
-        embed_finish(0)
-        for m in range(1, micros):
-            embed_tree(m)
+            opeak[:, span_rows] = jnp.max(peak.astype(jnp.float32).T, axis=0, keepdims=True)
+
+    with scope("p_embed"):
+
+        @pl.when(section > 0)
+        def _():
+            for m in range(micros):
+                embed_tree(m)
+
+        @pl.when(section == 0)
+        def _():
+            embed_tree(0)
+            embed_finish(0)
+            for m in range(1, micros):
+                embed_tree(m)
+
+    with scope("p_load"):
+        for load in loads:
+            load.wait()
+
+    with scope("p_wpeak"):
+
+        @pl.when(section > 0)
+        def _():
+            weight_peaks()
 
     def weight_copy(step):
         return remote(
@@ -325,6 +355,15 @@
             on_s.at[m, chunk, step],
             ag_r.at[m, chunk, me],
             (section + 1, col_peer(step) * minor + b),
+        )
+
+    def spread(m, chunk, step):
+        return remote(
+            xall.at[m, chunk, me],
+            xall.at[m, chunk, me],
+            col_s.at[m, chunk, step - 1],
+            ag_r.at[m, chunk, me],
+            peer(col_peer(step) * minor + b),
         )
 
     def kv_copy(m, step):
@@ -358,125 +397,155 @@
             peer(col_peer(order) * minor + b),
         )
 
-    def micro_step(m):
+    def consume(m, chunk):
+        @pl.loop(0, span // TILE)
+        def _(index):
+            cols = tile_at(index)
+            full = pl.ds(pl.multiple_of(chunk * span + index * TILE, TILE), TILE)
+            values = xall[m, chunk, :, :, cols].astype(jnp.float32).reshape(length, TILE)
+            square = values * values
+            total = square[:, :LANES]
+            for piece in range(1, TILE // LANES):
+                total += square[:, piece * LANES : (piece + 1) * LANES]
+            ssq[...] += total
+            gained = (values * gain[:, full]).astype(jnp.bfloat16)
+            acc_q[...] += jnp.dot(gained, wq[full, :], preferred_element_type=jnp.float32)
+            wkv = jnp.concatenate([wk[:, full], wv[:, full]], axis=0)
+            acc_kv[...] += lax.dot_general(
+                gained, wkv, (((1,), (1,)), ((), ())), preferred_element_type=jnp.float32
+            )
+
+    def first_cols(m, turn):
+        chunk = col_peer(-turn)
+        for sub in range(major):
+            piece = first_piece(m, chunk, b, sub)
+            remote(
+                piece,
+                piece,
+                fwd_s.at[m, turn, sub, 0],
+                ag_r.at[m, chunk, sub * minor + b],
+                peer(chunk * minor + b),
+            ).wait_recv()
+            for step in range(1, minor):
+                first_forward(m, turn, sub, step).start()
+
+    def first_rows(m, turn):
+        chunk = col_peer(-turn)
+        for sub in range(major):
+            for step in range(1, minor):
+                side = row_peer(step)
+                piece = first_piece(m, chunk, side, sub)
+                remote(
+                    piece,
+                    piece,
+                    fwd_s.at[m, turn, sub, step - 1],
+                    ag_r.at[m, chunk, sub * minor + side],
+                    peer(a * minor + side),
+                ).wait_recv()
+
+    def next_col(m, chunk, order):
+        origin = col_peer(-order) * minor + b
+        remote(
+            xall.at[m, chunk, origin],
+            xall.at[m, chunk, origin],
+            fwd_s.at[m, chunk, order, 0],
+            ag_r.at[m, chunk, origin],
+            (section - 1, origin),
+        ).wait_recv()
+        for step in range(1, minor):
+            forward(m, chunk, order, step).start()
+
+    def next_own(m, chunk):
+        next_col(m, chunk, 0)
+
+        @pl.when(section % 2 == 0)
+        def _():
+            for step in range(1, major):
+                spread(m, chunk, step).start()
+
+    def next_cols(m, chunk):
+        if chunk == 0:
+            next_own(m, 0)
+        if chunk < chunks - 1:
+            next_own(m, chunk + 1)
+        for order in range(1, major):
+            next_col(m, chunk, order)
+
+    def next_rows(m, chunk):
+        for order in range(major):
+            for step in range(1, minor):
+                side = row_peer(step)
+                origin = col_peer(-order) * minor + side
+                remote(
+                    xall.at[m, chunk, origin],
+                    xall.at[m, chunk, origin],
+                    fwd_s.at[m, chunk, order, step - 1],
+                    ag_r.at[m, chunk, origin],
+                    peer(a * minor + side),
+                ).wait_recv()
+
+    def clear():
         acc_q[...] = jnp.zeros_like(acc_q)
         acc_kv[...] = jnp.zeros_like(acc_kv)
         ssq[...] = jnp.zeros_like(ssq)
 
-        def consume(chunk):
-            @pl.loop(0, span // TILE)
-            def _(index):
-                cols = tile_at(index)
-                full = pl.ds(pl.multiple_of(chunk * span + index * TILE, TILE), TILE)
-                values = xall[m, chunk, :, :, cols].astype(jnp.float32).reshape(length, TILE)
-                square = values * values
-                total = square[:, :LANES]
-                for piece in range(1, TILE // LANES):
-                    total += square[:, piece * LANES : (piece + 1) * LANES]
-                ssq[...] += total
-                gained = (values * gain[:, full]).astype(jnp.bfloat16)
-                acc_q[...] += jnp.dot(gained, wq[full, :], preferred_element_type=jnp.float32)
-                wkv = jnp.concatenate([wk[:, full], wv[:, full]], axis=0)
-                acc_kv[...] += lax.dot_general(
-                    gained, wkv, (((1,), (1,)), ((), ())), preferred_element_type=jnp.float32
-                )
-
-        for turn in range(chunks + 1):
-            if turn < chunks:
-                with scope(f"p_col{turn}"):
-                    if turn > 0:
-
-                        @pl.when(section == 0)
-                        def _():
-                            chunk = col_peer(-turn)
-                            for sub in range(major):
-                                piece = first_piece(m, chunk, b, sub)
-                                remote(
-                                    piece,
-                                    piece,
-                                    fwd_s.at[m, turn, sub, 0],
-                                    ag_r.at[m, chunk, sub * minor + b],
-                                    peer(chunk * minor + b),
-                                ).wait_recv()
-                                for step in range(1, minor):
-                                    first_forward(m, turn, sub, step).start()
-
-                    @pl.when(section > 0)
-                    def _():
-                        for order in range(major):
-                            origin = col_peer(-order) * minor + b
-                            remote(
-                                xall.at[m, turn, origin],
-                                xall.at[m, turn, origin],
-                                fwd_s.at[m, turn, order, 0],
-                                ag_r.at[m, turn, origin],
-                                (section - 1, origin),
-                            ).wait_recv()
-                            for step in range(1, minor):
-                                forward(m, turn, order, step).start()
-
-            if turn > 0:
-                done = turn - 1
-                with scope(f"p_row{done}"):
+    def inverse_norm():
+        return lax.rsqrt(jnp.sum(ssq[...], axis=1, keepdims=True) / width + norm_eps)
+
+    def project(m):
+        inverse = inverse_norm()
+        kvbuf[m, me] = (acc_kv[...] * inverse).astype(jnp.bfloat16)
+        for step in range(1, count):
+            kv_copy(m, step).start()
+
+        for head in range(heads_here):
+            qrot[head] = rotated(acc_q[:, head * HEAD_DIM : (head + 1) * HEAD_DIM] * inverse)
+
+    clear()
+    for turn in range(chunks + 1):
+        if turn < chunks:
+            with scope(f"p_col{turn}"):
+                if turn > 0:
 
                     @pl.when(section == 0)
                     def _():
-                        chunk = col_peer(-done)
-                        for sub in range(major):
-                            for step in range(1, minor):
-                                side = row_peer(step)
-                                piece = first_piece(m, chunk, side, sub)
-                                remote(
-                                    piece,
-                                    piece,
-                                    fwd_s.at[m, done, sub, step - 1],
-                                    ag_r.at[m, chunk, sub * minor + side],
-                                    peer(a * minor + side),
-                                ).wait_recv()
-
-                    @pl.when(section > 0)
-                    def _():
-                        for order in range(major):
-                            for step in range(1, minor):
-                                side = row_peer(step)
-                                origin = col_peer(-order) * minor + side
-                                remote(
-                                    xall.at[m, done, origin],
-                                    xall.at[m, done, origin],
-                                    fwd_s.at[m, done, order, step - 1],
-                                    ag_r.at[m, done, origin],
-                                    peer(a * minor + side),
-                                ).wait_recv()
-
-                with scope(f"p_qkv{done}"):
-                    consume(done * later + (1 - later) * col_peer(-done))
-
-        with scope("p_scale"):
-            inverse = lax.rsqrt(jnp.sum(ssq[...], axis=1, keepdims=True) / width + norm_eps)
-            kvbuf[m, me] = (acc_kv[...] * inverse).astype(jnp.bfloat16)
-            for step in range(1, count):
-                kv_copy(m, step).start()
-
-            @pl.when(jnp.logical_and(section == 0, m < micros - 1))
-            def _():
-                embed_finish(m + 1)
-
-            queries = [
-                rotated(acc_q[:, head * HEAD_DIM : (head + 1) * HEAD_DIM] * inverse)
-                for head in range(heads_here)
-            ]
-
+                        first_cols(0, turn)
+
+                @pl.when(section > 0)
+                def _():
+                    next_cols(0, turn)
+
+        if turn > 0:
+            done = turn - 1
+            with scope(f"p_row{done}"):
+
+                @pl.when(section == 0)
+                def _():
+                    first_rows(0, done)
+
+                @pl.when(section > 0)
+                def _():
+                    next_rows(0, done)
+
+            with scope(f"p_qkv{done}"):
+                consume(0, done * later + (1 - later) * col_peer(-done))
+    with scope("p_project"):
+        project(0)
+
+    def micro_step(m):
+        more = m < micros - 1
         with scope("p_actpeak"):
-            for chunk in range(chunks):
-
-                @pl.loop(0, span // TILE)
-                def _(index):
-                    cols = tile_at(index)
-                    full = pl.ds(pl.multiple_of(chunk * span + index * TILE, TILE), TILE)
-                    values = xall[m, chunk, :, :, cols].astype(jnp.float32).reshape(length, TILE)
-                    peak = jnp.max(jnp.abs(values * inverse), axis=0, keepdims=True)
-                    peak = (peak * jnp.abs(gain[:, full])).astype(jnp.bfloat16)
-                    act_out[:, full] = jnp.maximum(act_out[:, full], peak.astype(jnp.float32))
+            inverse = inverse_norm()
+
+            @pl.loop(0, width // TILE)
+            def _(index):
+                full = tile_at(index)
+                chunk = index // (span // TILE)
+                cols = tile_at(index % (span // TILE))
+                values = xall[m, chunk, :, :, cols].astype(jnp.float32).reshape(length, TILE)
+                peak = jnp.max(jnp.abs(values * inverse), axis=0, keepdims=True)
+                peak = (peak * jnp.abs(gain[:, full])).astype(jnp.bfloat16)
+                act_peak[:, full] = jnp.maximum(act_peak[:, full], peak.astype(jnp.float32))
 
         with scope("p_kvwait"):
             for step in range(1, count):
@@ -488,6 +557,11 @@
                     kv_r.at[m, origin],
                     peer(origin),
                 ).wait_recv()
+
+        @pl.when(jnp.logical_and(more, section == 0))
+        def _():
+            embed_finish(m + 1)
+
         with scope("p_attn"):
             for group in range(KV_HEADS):
                 blocks = [
@@ -504,7 +578,7 @@
                 else:
                     group = lax.rem(me * heads_here + head, KV_HEADS)
                 scores = lax.dot_general(
-                    queries[head],
+                    qrot[head],
                     krot[group],
                     (((1,), (1,)), ((), ())),
                     preferred_element_type=jnp.float32,
@@ -517,7 +591,13 @@
                 cols = pl.ds(head * HEAD_DIM, HEAD_DIM)
                 att[:, cols] = mixed
                 peak = jnp.max(jnp.abs(mixed.astype(jnp.float32)), axis=0, keepdims=True)
-                head_out[:, cols] = jnp.maximum(head_out[:, cols], peak)
+                head_peak[:, cols] = jnp.maximum(head_peak[:, cols], peak)
+
+        with scope("p_gate"):
+
+            @pl.when(jnp.logical_and(m > 0, section % 2 == 0))
+            def _():
+                pl.semaphore_wait(gate, 1)
 
         with scope("p_oproj"):
             for chunk in range(chunks):
@@ -583,18 +663,65 @@
 
             @pl.when(section < sections - 1)
             def _():
-                for step in range(major):
+                onward(m, chunk, 0).start()
+
+            @pl.when(jnp.logical_and(section < sections - 1, section % 2 == 0))
+            def _():
+                for step in range(1, major):
                     onward(m, chunk, step).start()
+
+        @pl.when(more)
+        def _():
+            clear()
+
+        @pl.when(jnp.logical_and(more, section == 0))
+        def _():
+            for turn in range(1, major):
+                first_cols(m + 1, turn)
 
         for chunk in range(chunks + 1):
             if chunk < chunks:
                 with scope(f"p_rs1_{chunk}"):
                     first_sum(chunk)
+            if chunk == 1:
+
+                @pl.when(jnp.logical_and(more, section % 2 == 1))
+                def _():
+                    pl.semaphore_signal(
+                        gate, inc=1, device_id=(section - 1, me), device_id_type=MESH
+                    )
+
             if chunk > 0:
                 with scope(f"p_rs2_{chunk - 1}"):
                     second_sum(chunk - 1)
 
-        @pl.when(m == 0)
+        with scope("p_nextfirst"):
+
+            @pl.when(jnp.logical_and(more, section == 0))
+            def _():
+                @pl.loop(0, major)
+                def _(turn):
+                    first_rows(m + 1, turn)
+                    consume(m + 1, col_peer(-turn))
+
+        for turn in range(chunks + 1):
+            with scope(f"p_next{turn}"):
+
+                @pl.when(jnp.logical_and(more, section > 0))
+                def _():
+                    if turn < chunks:
+                        next_cols(m + 1, turn)
+                    if turn > 0:
+                        next_rows(m + 1, turn - 1)
+                        consume(m + 1, turn - 1)
+
+        with scope("p_project"):
+
+            @pl.when(more)
+            def _():
+                project(m + 1)
+
+        @pl.when(jnp.logical_and(m == 0, section > 0))
         def _():
             for step in range(1, count):
                 weight_copy(step).start()
@@ -603,7 +730,13 @@
     def _(m):
         micro_step(m)
 
-    with scope("p_wpwait"):
+    @pl.when(section == 0)
+    def _():
+        weight_peaks()
+        for step in range(1, count):
+            weight_copy(step).start()
+
+    with scope("p_scales"):
         peak = wpeak[...]
         for step in range(1, count):
             origin = lax.rem(me + step, count)
@@ -611,7 +744,8 @@
                 wpeak, wpbuf.at[origin], wp_s.at[step - 1], wp_r.at[origin], peer(origin)
             ).wait_recv()
             peak = jnp.maximum(peak, wpbuf[origin])
-        wpeak_out[...] = peak
+        scale_in[...] = smoothing(act_peak[...], peak, alpha[...])
+        scale_out[...] = smoothing(head_peak[...], opeak[...], alpha[...])
 
     with scope("p_sends"):
         for level, distance in enumerate(distances):
@@ -643,8 +777,19 @@
             @pl.when(section < sections - 1)
             def _():
                 for chunk in range(chunks):
-                    for step in range(major):
+                    onward(m, chunk, 0).wait_send()
+
+            @pl.when(jnp.logical_and(section < sections - 1, section % 2 == 0))
+            def _():
+                for chunk in range(chunks):
+                    for step in range(1, major):
                         onward(m, chunk, step).wait_send()
+
+            @pl.when(jnp.logical_and(section > 0, section % 2 == 0))
+            def _():
+                for chunk in range(chunks):
+                    for step in range(1, major):
+                        spread(m, chunk, step).wait_send()
 
             for step in range(1, count):
                 kv_copy(m, step).wait_send()
@@ -658,7 +803,7 @@
             weight_copy(step).wait_send()
 
 
-def run_layers(sections, count, picked, gain, wq, wk, wv, wo, cos2, sin2):
+def run_layers(sections, count, picked, gain, wq, wk, wv, wo, cos2, sin2, alpha):
     major, minor = grid_of(count)
     micros, _, rows, feats = picked.shape
     width = feats * count
@@ -670,6 +815,7 @@
     span = width // chunks
     bf16, f32 = jnp.bfloat16, jnp.float32
     vmem = pl.BlockSpec(memory_space=pltpu.VMEM)
+    anywhere = pl.BlockSpec(memory_space=pltpu.HBM)
     dma = pltpu.SemaphoreType.DMA
     return pl.pallas_call(
         functools.partial(layers_kernel, sections, count),
@@ -677,12 +823,18 @@
             jax.ShapeDtypeStruct((micros, rows, width), bf16),
             jax.ShapeDtypeStruct((1, width), f32),
             jax.ShapeDtypeStruct((1, query_cols), f32),
-            jax.ShapeDtypeStruct((1, width), f32),
-            jax.ShapeDtypeStruct((1, query_cols), f32),
         ),
-        in_specs=[vmem] * 8,
-        out_specs=(vmem,) * 5,
+        in_specs=[vmem] * 2 + [anywhere] * 4 + [vmem] * 3,
+        out_specs=(vmem,) * 3,
         scratch_shapes=[
+            pltpu.VMEM(wq.shape, bf16),
+            pltpu.VMEM(wk.shape, bf16),
+            pltpu.VMEM(wv.shape, bf16),
+            pltpu.VMEM(wo.shape, bf16),
+            pltpu.VMEM((1, width), f32),
+            pltpu.VMEM((1, query_cols), f32),
+            pltpu.VMEM((1, query_cols), f32),
+            pltpu.VMEM((query_cols // HEAD_DIM, length, HEAD_DIM), bf16),
             pltpu.VMEM((levels, micros, count, rows, feats), bf16),
             pltpu.VMEM((micros, count, rows, feats), bf16),
             pltpu.VMEM((micros, chunks, count, rows, span), bf16),
@@ -700,6 +852,7 @@
             pltpu.VMEM((chunks, rows, span), f32),
             pltpu.VMEM((1, width), f32),
             pltpu.VMEM((count, 1, width), f32),
+            dma((4,)),
             dma((levels, micros)),
             dma((levels, micros)),
             dma((micros, major, major - 1)),
@@ -714,15 +867,74 @@
             dma((micros, chunks, major)),
             dma((count - 1,)),
             dma((count,)),
+            pltpu.SemaphoreType.REGULAR,
         ],
         compiler_params=pltpu.CompilerParams(
             collective_id=0, has_side_effects=True, vmem_limit_bytes=VMEM_MIB * 1024 * 1024
         ),
         name="layers",
-    )(picked, gain, wq, wk, wv, wo, cos2, sin2)
-
-
-VMEM_MIB = 24
+    )(picked, gain, wq, wk, wv, wo, cos2, sin2, alpha)
+
+
+VMEM_MIB = 40
+
+
+PACK = 8
+GROUP = 16
+
+
+def pick_kernel(starts, marks, table, picked, tiles, sem):
+    total = picked.shape[0]
+
+    def fetch(token):
+        start = pl.multiple_of(starts[token] * PACK, PACK)
+        return pltpu.make_async_copy(
+            table.at[pl.ds(start, PACK), :],
+            tiles.at[pl.ds(pl.multiple_of(token * PACK, PACK), PACK), :],
+            sem,
+        )
+
+    @pl.loop(0, total, unroll=8)
+    def _(token):
+        fetch(token).start()
+
+    pltpu.make_async_copy(tiles, tiles, sem).wait()
+
+    @pl.loop(0, total // GROUP)
+    def _(group):
+        here = pl.ds(pl.multiple_of(group * GROUP, GROUP), GROUP)
+        depth = GROUP * PACK
+        columns = lax.broadcasted_iota(jnp.int32, (GROUP, depth), 1)
+        chosen = jnp.where(columns == marks[here, :], 1.0, 0.0).astype(jnp.bfloat16)
+        block = tiles[pl.ds(pl.multiple_of(group * depth, depth), depth), :]
+        picked[here, :] = jnp.dot(chosen, block, preferred_element_type=jnp.float32).astype(
+            jnp.bfloat16
+        )
+
+
+def pick_rows(local_ids, table):
+    total = local_ids.shape[0]
+    vocab_rows, feats = table.shape
+    inside = (local_ids >= 0) & (local_ids < vocab_rows)
+    clipped = jnp.clip(local_ids, 0, vocab_rows - 1)
+    place = (jnp.arange(total, dtype=jnp.int32) % GROUP) * PACK + clipped % PACK
+    marks = jnp.where(inside, place, -1).reshape(total, 1)
+    return pl.pallas_call(
+        pick_kernel,
+        out_shape=jax.ShapeDtypeStruct((total, feats), jnp.bfloat16),
+        in_specs=[
+            pl.BlockSpec(memory_space=pltpu.SMEM),
+            pl.BlockSpec(memory_space=pltpu.VMEM),
+            pl.BlockSpec(memory_space=pltpu.HBM),
+        ],
+        out_specs=pl.BlockSpec(memory_space=pltpu.VMEM),
+        scratch_shapes=[
+            pltpu.VMEM((total * PACK, feats), jnp.bfloat16),
+            pltpu.SemaphoreType.DMA,
+        ],
+        compiler_params=pltpu.CompilerParams(vmem_limit_bytes=36 * 1024 * 1024),
+        name="pick",
+    )(clipped // PACK, marks, table)
 
 
 def shards(token_ids, alpha_num, embed_table, norm_gain, w_query, w_key, w_value, w_out):
@@ -731,16 +943,15 @@
     section_index = lax.axis_index("section")
     micros, length = token_ids.shape
     vocab_rows, feats = embed_table.shape
-    local_ids = token_ids - section_index * vocab_rows
-    inside = (local_ids >= 0) & (local_ids < vocab_rows)
-    picked = jnp.take(embed_table, jnp.clip(local_ids, 0, vocab_rows - 1), axis=0)
-    picked = jnp.where(inside[:, :, None], picked, jnp.zeros_like(picked))
+    local_ids = (token_ids - section_index * vocab_rows).reshape(-1)
+    picked = pick_rows(local_ids, embed_table)
     picked = picked.reshape(micros, tp_count, length // tp_count, feats)
     w_query, w_key, w_value, w_out = w_query[0], w_key[0], w_value[0], w_out[0]
     cosine, sine = rope_tables(length, HEAD_DIM)
     cos2 = jnp.concatenate([cosine, cosine], axis=1)
     sin2 = jnp.concatenate([-sine, sine], axis=1)
-    stored, act_peak, head_peak, weight_peak, out_peak = run_layers(
+    alpha_exp = (alpha_num[0].astype(jnp.float32) / 10.0).reshape(1, 1)
+    stored, scale_in, scale_out = run_layers(
         section_count,
         tp_count,
         picked,
@@ -751,18 +962,16 @@
         w_out,
         cos2,
         sin2,
+        alpha_exp,
     )
-    alpha_exp = alpha_num[0].astype(jnp.float32) / 10.0
-    scale_in = smoothing(act_peak[0], weight_peak[0], alpha_exp)
-    scale_out = smoothing(head_peak[0], out_peak[0], alpha_exp)
 
     def smoothed(weights):
-        return (weights.astype(jnp.float32) * scale_in[:, None]).astype(jnp.bfloat16)
+        return (weights.astype(jnp.float32) * scale_in[0][:, None]).astype(jnp.bfloat16)
 
     return (
         stored[None],
-        scale_in[None],
-        scale_out[None],
+        scale_in,
+        scale_out,
         smoothed(w_query)[None],
         smoothed(w_key)[None],
         smoothed(w_value)[None],

time: 306 us -> 282 us (0.922)
  local copies, waits for them, and re-layouts: 20.2 us -> 2.34 us
  Pallas kernels: 276 us -> 270 us
    pallas_call x1, Pallas kernels: 276 us -> 258 us  [run_layers(): pl.pallas_call(functools.partial(layers_kernel, sections, count), out_sha...]
    pallas_call x0 -> x1, Pallas kernels: none -> 12.3 us  [pick_rows(): pl.pallas_call(pick_kernel, out_shape=jax.ShapeDtypeStruct((total, feats)...]
    gather x1 -> x0, local copies, waits for them, and re-layouts: 9.24 us -> none  [shards(): jnp.take(embed_table, jnp.clip(local_ids, 0, vocab_rows - 1), axis=0)]
    unnamed x13 -> x15, local copies, waits for them, and re-layouts: 10.8 us -> 2.2 us
where the time goes in v2:
time: 282 us
  Pallas kernels  270 us (96%)
  other arithmetic  7.79 us (3%)
    pallas_call x1, Pallas kernels, run_layers(): pl.pallas_call(functools.partial(layers_kernel, sections, count), out_sha...  258 us
    pallas_call x1, Pallas kernels, pick_rows(): pl.pallas_call(pick_kernel, out_shape=jax.ShapeDtypeStruct((total, feats)...  12.3 us
    convert_element_type x2, other arithmetic, smoothed(): (weights.astype(jnp.float32) * scale_in[0][:, None]).astype(jnp.bfloat16)  5.95 us

profile of v2, /device:TPU:5, one launch (start us, length us, event | category | flops | bytes accessed | tf_op | source)
XLA Modules:
  0.0 281.7 jit_solution(12391665222847290361)
XLA Ops:
  1.3 0.7 and_bitcast_fusion
  2.0 0.7 and_select_fusion
  2.7 0.2 copy.19
  2.9 0.1 copy.14
  3.0 0.1 fusion.2.marks
  3.1 0.0 slice-start
  3.1 0.3 fusion.9
  3.4 0.1 pad_maximum_fusion
  3.5 0.0 slice-start.1
  3.5 0.0 copy-start
  3.5 0.0 copy-start.1
  3.5 0.0 copy-start.2
  3.5 12.3 %pick.1 = bf16[256,1024]{1,0:T(8,128)(2,1)S(1)} custom-call(s32[256]{0:T(256)S(1)} %get-tuple-element.12.starts, s32[256,1]{1,0:T(8,128)S(1)} %fusion.2.marks, bf16[16384,1024]{1,0:T(8,128)(2,1)} %table.1), custom_call_target="tpu_custom_call" | custom-call | tf_op jit(solution)/shard_map/pick/pallas_call | solution.py:922
  15.9 0.0 slice-done
  15.9 0.0 slice-done.1
  15.9 0.0 copy-done
  15.9 0.0 copy-done.1
  15.9 0.0 copy-done.2
  15.9 257.8 %layers.1 = (bf16[2,16,8192]{2,1,0:T(8,128)(2,1)S(1)}, f32[1,8192]{1,0:T(1,128)S(1)}, f32[1,512]{1,0:T(1,128)S(1)}) custom-call(bf16[2,8,16,1024]{3,2,1,0:T(8,128)(2,1)S(1)} %bitcast.34, f32[1,8192]{1,0:T(1,128)S(1)} %copy-done.2, bf16[8192,512]{1,0:T(8,128)(2,1)S(1)} %bitcast.31, bf16[64,8192]{1,0:T(8,128)(2,1)S(1)} %bitcast.32, ...), custom_call_target="tpu_custom_call" | custom-call | tf_op jit(solution)/shard_map/layers/pallas_call | solution.py:820
  273.8 1.7 multiply_convert_fusion.1
  275.5 4.2 %multiply_convert_fusion = bf16[1,8192,512]{2,1,0:T(8,128)(2,1)} fusion(bf16[1,8192,512]{2,1,0:T(8,128)(2,1)S(1)} %bitcast.30, f32[8192]{0:T(1024)S(1)} %bitcast.37), kind=kLoop, calls=%fused_computation | loop fusion | flops 12582912 | bytes 16809984 | tf_op jit(solution)/shard_map/convert_element_type | solution.py:969
  279.7 0.8 copy.26
  280.5 0.6 copy.27
  281.1 0.6 copy.28
  (3 shorter events, 0.0 us)
Async XLA Ops:
  3.1 12.8 %slice-start = ((s8[8388608]{0:T(1024)(128)(4,1)}), s8[4194304]{0:T(1024)(128)(4,1)S(1)}, s32[]{:S(2)}) async-start(s8[8388608]{0:T(1024)(128)(4,1)} %bitcast.29), calls=%async_computation | async-start | bytes 8388608
  3.5 12.4 %slice-start.1 = ((s8[8388608]{0:T(1024)(128)(4,1)}), s8[4194304]{0:T(1024)(128)(4,1)S(1)}, s32[]{:S(2)}) async-start(s8[8388608]{0:T(1024)(128)(4,1)} %bitcast.29), calls=%async_computation.1 | async-start | bytes 8388608
  3.5 12.4 %copy-start = (bf16[1,8192,64]{1,2,0:T(8,128)(2,1)S(1)}, bf16[1,8192,64]{1,2,0:T(8,128)(2,1)}, u32[]{:S(2)}) copy-start(bf16[1,8192,64]{1,2,0:T(8,128)(2,1)} %param.13) | copy-start | bytes 3145732
  3.5 12.4 %copy-start.1 = (bf16[1,8192,64]{1,2,0:T(8,128)(2,1)S(1)}, bf16[1,8192,64]{1,2,0:T(8,128)(2,1)}, u32[]{:S(2)}) copy-start(bf16[1,8192,64]{1,2,0:T(8,128)(2,1)} %param.14) | copy-start | bytes 3145732
  3.5 12.4 %copy-start.2 = (f32[1,8192]{1,0:T(1,128)S(1)}, f32[1,8192]{1,0:T(1,128)}, u32[]{:S(2)}) copy-start(f32[1,8192]{1,0:T(1,128)} %gain.1) | copy-start | bytes 98308
